TPU v7x, 256 devices: a whole 4x4x8 slice. The times are simulated.
256 devices in a mesh: dp: 128 (over z_hi, x, y, core), tensor: 2 (over z_lo).
Axes of the slice: x: 4, y: 4, z: 8 (z_hi: 4, z_lo: 2; z = z_hi * 2 + z_lo), core: 2. Of those that a mesh axis runs over, the one named last changes fastest.
Arguments:
- tokens: bfloat16 [16384, 1792], P('dp'), may hold values from -6 to 6
- targets: bfloat16 [16384, 1792], P('dp'), may hold values from -6 to 6
- live_mask: int32 [16384], P('dp'), may hold values from 0 to 1, as said below
- up_weight: bfloat16 [1792, 7168], P('dp', 'tensor'), may hold values from -0.125 to 0.125
- down_weight: bfloat16 [1792, 7168], P('dp', 'tensor'), may hold values from -0.0625 to 0.0625
- probe_rows: int32 [1792], replicated, may hold values from 0 to 16777215
- probe_cols: int32 [7168], P('tensor'), may hold values from 0 to 16777215
- moment: float32 [1792, 512], P('dp', 'tensor'), may hold values from 0.01 to 1
Outputs:
- hess_diag: float32 [1792, 512], P('dp', 'tensor')
- second_moment: float32 [1792, 512], P('dp', 'tensor')
- mean_loss: float32 [], replicated
Inputs may be any that keep to these rules, and one draw needn't show every extreme that they name: In every aligned block of 128 tokens the first token has live_mask 1.
All inputs are finite; a program needn't handle non-finite values.
Results may differ from a plain program's by a relative error of at most 0.0023.
Values may be sent and summed in bfloat16 or wider, within the bound.
No kernel may reach another device: no remote copies, remote signals or barrier semaphores. Data moves between devices by JAX's collectives and lax.ppermute only.
A program may use at most 128 MiB of HBM per device.

v0:
```python
import jax
import jax.numpy as jnp
from jax import lax
from jax.sharding import Mesh
from jax.sharding import PartitionSpec as P

BLOCK = 14
DP = ("dp_0", "dp_1", "dp_2", "dp_3")
DP_TENSOR = ("dp_0", "dp_1", "dp_2", "dp_3", "tensor")
gelu_coef = 0.7978845608028654
cubic_coef = 0.044715
beta_two = 0.999


def sent_to_all(shard, axis):
    copies = jnp.broadcast_to(shard, (lax.axis_size(axis), *shard.shape))
    return lax.all_to_all(copies, axis, split_axis=0, concat_axis=0, tiled=True)


def over_copies(shard, axis):
    everything = sent_to_all(shard, axis)
    return jnp.sum(everything, axis=0)


def together(arrays, axis):
    line, at, done = (jnp.concatenate([a.reshape(-1) for a in arrays]), 0, [])
    total = over_copies(line, axis)
    for a in arrays:
        done.append(total[at : at + a.size].reshape(a.shape))
        at += a.size
    return tuple(done)


def cut_along(shard, dim, count):
    before, after = (shard.shape[:dim], shard.shape[dim + 1 :])
    return jnp.moveaxis(shard.reshape(*before, count, -1, *after), dim, 0)


def sent_and_summed(shard, axis, dim):
    count = lax.axis_size(axis)
    tiles = lax.all_to_all(cut_along(shard, dim, count), axis, 0, 0, tiled=True)
    return jnp.sum(tiles, axis=0)


def sum_in_two_steps(shard, axes, dim):
    far, near = axes
    own = sent_and_summed(cut_along(shard, dim, lax.axis_size(far)), near, dim + 1)
    return jnp.sum(lax.all_to_all(own, far, 0, 0, tiled=True), axis=0)


def one_axis_at_a_time(shard, axes):
    for axis in axes:
        shard = lax.psum(shard, axis)
    return shard


def probe_signs(row_keys, col_keys):
    hashed = jnp.bitwise_xor(row_keys[:, None] * 747796405, col_keys[None, :])
    hashed = jnp.bitwise_xor(hashed, jnp.right_shift(hashed, 15) & 131071)
    hashed = hashed * 695872825
    hashed = jnp.bitwise_xor(hashed, jnp.right_shift(hashed, 13) & 524287)
    hashed = hashed * 739982445
    hashed = jnp.bitwise_xor(hashed, jnp.right_shift(hashed, 16) & 65535)
    parity = jnp.right_shift(hashed, 11) & 1
    return (2 * parity - 1).astype(jnp.bfloat16)


def gelu_parts(preact):
    tanh_arg = gelu_coef * (preact + cubic_coef * preact * preact * preact)
    tanh_val = jnp.tanh(tanh_arg)
    sech_sq = 1.0 - tanh_val * tanh_val
    arg_slope = gelu_coef * (1.0 + 3.0 * cubic_coef * preact * preact)
    arg_curve = gelu_coef * 6.0 * cubic_coef * preact
    gelu_value = 0.5 * preact * (1.0 + tanh_val)
    gelu_slope = 0.5 * (1.0 + tanh_val) + 0.5 * preact * sech_sq * arg_slope
    gelu_curve = sech_sq * (
        arg_slope - preact * tanh_val * arg_slope * arg_slope + 0.5 * preact * arg_curve
    )
    return (gelu_value, gelu_slope, gelu_curve)


def body(tokens, targets, live_mask, up_weight, down_weight, probe_rows, probe_cols, moment):
    tok_count = tokens.shape[0]
    ff_local = up_weight.shape[1]
    own_rows = up_weight.shape[0]
    tensor_count = lax.axis_size("tensor")
    live_rows = live_mask.astype(jnp.float32)
    local_count = jnp.sum(live_rows) * (1.0 / tensor_count)
    all_signs = probe_signs(probe_rows, probe_cols)
    columns = tokens
    sign_rows = all_signs
    joined = jnp.concatenate([lax.all_gather(up_weight, DP, axis=0, tiled=True), sign_rows], axis=1)
    both_pre = jnp.dot(columns, joined, preferred_element_type=jnp.float32)
    preact = both_pre[:, :ff_local]
    tangent = both_pre[:, ff_local:]
    full_down = lax.all_gather(down_weight, DP, axis=0, tiled=True)
    gelu_value, gelu_slope, gelu_curve = gelu_parts(preact)
    hidden = gelu_value.astype(jnp.bfloat16)
    hidden_dir = (gelu_slope * tangent).astype(jnp.bfloat16)
    stacked = jnp.concatenate([hidden, hidden_dir], axis=0)
    projected = jnp.einsum("tf,df->td", stacked, full_down, preferred_element_type=jnp.float32)
    outputs, out_dir = together((projected[:tok_count], projected[tok_count:]), "tensor")
    diff = outputs - targets.astype(jnp.float32)
    weighted = live_rows[:, None] * diff
    local_loss = jnp.sum(weighted * diff) * (1.0 / tensor_count)
    residual = weighted.astype(jnp.bfloat16)
    residual_dir = (live_rows[:, None] * out_dir).astype(jnp.bfloat16)
    back_prod = jnp.dot(
        jnp.concatenate([residual, residual_dir], axis=0),
        full_down,
        preferred_element_type=jnp.float32,
    )
    grad_h = back_prod[:tok_count]
    grad_dir = back_prod[tok_count:]
    chain_grad = (grad_dir * gelu_slope + grad_h * gelu_curve * tangent).astype(jnp.bfloat16)
    columns = tokens
    product = jnp.einsum("tr,tf->rf", columns, chain_grad, preferred_element_type=jnp.float32)
    sign_rows = all_signs
    hutch_terms = sign_rows.astype(jnp.float32) * product
    own_share = sum_in_two_steps(
        hutch_terms.reshape(own_rows * lax.axis_size(DP), ff_local // BLOCK, BLOCK).mean(axis=-1),
        (("dp_0", "dp_1", "dp_2"), "dp_3"),
        0,
    )
    loss_sum, total_count = (
        one_axis_at_a_time(local_loss, DP_TENSOR),
        one_axis_at_a_time(local_count, DP_TENSOR),
    )
    hess_diag = own_share / total_count
    second_moment = beta_two * moment + (1.0 - beta_two) * hess_diag * hess_diag
    mean_loss = loss_sum / (2.0 * total_count)
    return (hess_diag, second_moment, mean_loss)


def solution(mesh):
    torus = Mesh(
        mesh.devices.reshape(4, 4, 4, 2, mesh.shape["tensor"]),
        ("dp_0", "dp_1", "dp_2", "dp_3", "tensor"),
    )
    placed = (
        P(DP, None),
        P(DP, None),
        P(DP),
        P(DP, "tensor"),
        P(DP, "tensor"),
        P(),
        P("tensor"),
        P(DP, "tensor"),
    )
    return jax.shard_map(
        body,
        mesh=torus,
        in_specs=placed,
        out_specs=(P(DP, "tensor"), P(DP, "tensor"), P()),
        check_vma=False,
    )
```

profile of v0, /device:TPU:1, one launch (start us, length us, event | category | flops | bytes accessed | tf_op | source)
XLA Modules:
  0.0 491.9 jit_solution(3638978809061497128)
XLA Ops:
  9.4 15.8 %add_convert_fusion = bf16[1792,3584]{0,1:T(8,128)(2,1)} fusion(s32[3584]{0:T(1024)} %param.14, s32[1792]{0:T(1024)S(1)} %broadcast_multiply_fusion.1), kind=kLoop, calls=%fused_computation.13 | loop fusion | flops 109182976 | bytes 12866560 | tf_op jit(solution)/shard_map/convert_element_type | solution.py:65
  25.2 99.8 %all-gather.5.cloned.1.call-done = bf16[128,14,3584]{2,1,0:T(8,128)(2,1)} async-done(((bf16[1,14,3584]{2,1,0:T(8,128)(2,1)}), bf16[128,14,3584]{2,1,0:T(8,128)(2,1)}) %all-gather.5.cloned.1.call-update) | async-done | bytes 12845072 | tf_op jit(solution)/shard_map/all_gather | solution.py:92
  125.0 16.8 %reshape.48 = bf16[1792,3584]{1,0:T(8,128)(2,1)} reshape(bf16[128,14,3584]{2,1,0:T(8,128)(2,1)} %all-gather.5.cloned.1.call-done) | data formatting | bytes 25690112
  141.9 17.9 %copy.27 = bf16[1792,3584]{0,1:T(8,128)(2,1)} copy(bf16[1792,3584]{1,0:T(8,128)(2,1)} %reshape.48) | data formatting | bytes 25690112
  159.8 15.2 %fusion.10 = f32[128,7168]{1,0:T(8,128)} fusion(bf16[128,1792]{1,0:T(8,128)(2,1)S(1)} %copy-done, bf16[1792,3584]{0,1:T(8,128)(2,1)} %add_convert_fusion, bf16[1792,3584]{0,1:T(8,128)(2,1)} %copy.27), kind=kOutput, calls=%fused_computation.14 | convolution fusion | flops 3339714560 | bytes 29818880 | tf_op jit(solution)/shard_map/dot_general | solution.py:93
  175.0 3.3 multiply_convert_fusion.1
  178.3 57.5 %all-gather.7.cloned.1.call-done = bf16[128,14,3584]{2,1,0:T(8,128)(2,1)} async-done(((bf16[1,14,3584]{2,1,0:T(8,128)(2,1)}), bf16[128,14,3584]{2,1,0:T(8,128)(2,1)}) %all-gather.7.cloned.1.call-update) | async-done | bytes 12845072 | tf_op jit(solution)/shard_map/all_gather | solution.py:96
  235.8 16.8 %reshape.50 = bf16[1792,3584]{1,0:T(8,128)(2,1)} reshape(bf16[128,14,3584]{2,1,0:T(8,128)(2,1)} %all-gather.7.cloned.1.call-done) | data formatting | bytes 25690112
  252.6 7.0 %fusion.23 = f32[256,1792]{1,0:T(8,128)S(1)} fusion(bf16[1792,3584]{1,0:T(8,128)(2,1)} %reshape.50, bf16[128,3584]{1,0:T(8,128)(2,1)S(1)} %get-tuple-element.16, bf16[128,3584]{1,0:T(8,128)(2,1)S(1)} %get-tuple-element.15), kind=kOutput, calls=%fused_computation.29 | convolution fusion | flops 3292004352 | bytes 16515072 | tf_op jit(solution)/shard_map/tf,df->td/dot_general | solution.py:101
  260.1 3.3 broadcast_in_dim.2
  263.3 5.7 %all-to-all-start = ((f32[2,1,458752]{2,1,0:T(1,128)}), f32[2,1,458752]{2,1,0:T(1,128)}, u32[]{:S(2)}, u32[]{:S(2)}) async-start(f32[2,1,458752]{2,1,0:T(1,128)} %broadcast_in_dim.2), calls=%async_computation | async-start | bytes 7340032 | tf_op jit(solution)/shard_map/all_to_all | solution.py:17
  269.1 41.4 %all-to-all-done = f32[2,1,458752]{2,1,0:T(1,128)} async-done(((f32[2,1,458752]{2,1,0:T(1,128)}), f32[2,1,458752]{2,1,0:T(1,128)}, u32[]{:S(2)}, u32[]{:S(2)}) %all-to-all-start) | async-done | bytes 3670048 | tf_op jit(solution)/shard_map/all_to_all | solution.py:17
  310.5 18.1 %reduce_sum.54 = f32[458752]{0:T(1024)S(1)} reduce(f32[2,1,458752]{2,1,0:T(1,128)} %all-to-all-done, f32[]{:T(128)} %constant.20.clone.1), dimensions={0,1}, to_apply=%region_0.0 | reduce | flops 458752 | bytes 5505028 | tf_op jit(solution)/shard_map/reduce_sum | solution.py:22
  329.7 1.3 slice.49
  331.2 2.0 fusion.27
  333.1 6.7 %fusion.29 = f32[256,3584]{1,0:T(8,128)S(1)} fusion(bf16[1792,3584]{1,0:T(8,128)(2,1)} %reshape.50, bf16[128,1792]{1,0:T(8,128)(2,1)S(1)} %get-tuple-element.23, bf16[128,1792]{1,0:T(8,128)(2,1)S(1)} %get-tuple-element.22), kind=kOutput, calls=%fused_computation.41 | convolution fusion | flops 3290169344 | bytes 17432576 | tf_op jit(solution)/shard_map/dot_general | solution.py:108
  339.8 17.9 %bitcast_multiply_fusion = f32[1792,3584]{0,1:T(8,128)} fusion(bf16[128,1792]{1,0:T(8,128)(2,1)S(1)} %copy-done, s32[3584]{0:T(1024)S(1)} %copy-done.3, s32[1792]{0:T(1024)S(1)} %broadcast_multiply_fusion.1, f32[256,3584]{1,0:T(8,128)S(1)} %fusion.29, f32[128,7168]{1,0:T(8,128)S(1)} %copy-done.2), kind=kOutput, calls=%fused_computation.12 | convolution fusion | flops 1779957760 | bytes 33510400 | tf_op jit(solution)/shard_map/tr,tf->rf/dot_general | solution.py:117
  357.7 26.7 %reshape.46 = f32[1792,256,14]{0,2,1:T(8,128)} reshape(f32[1792,3584]{0,1:T(8,128)} %bitcast_multiply_fusion) | data formatting | bytes 51380224 | tf_op jit(solution)/shard_map/reshape | solution.py:121
  384.4 13.6 %reduce_sum.55 = f32[1792,256]{0,1:T(8,128)} reduce(f32[1792,256,14]{0,2,1:T(8,128)} %reshape.46, f32[]{:T(128)} %constant.20.clone.1), dimensions={2}, to_apply=%region_1.0 | reduce | flops 5963776 | bytes 27525124 | tf_op jit(solution)/shard_map/reduce_sum | solution.py:121
  398.0 1.7 broadcast_multiply_fusion
  399.7 1.7 copy.29
  401.4 1.6 div.19
  403.0 1.1 copy.30
  404.1 6.1 %all_to_all.16 = f32[2,64,14,256]{3,1,2,0:T(8,128)S(1)} all-to-all(f32[2,64,14,256]{3,1,2,0:T(8,128)S(1)} %copy.30), channel_id=1, replica_groups=mesh['dp_0'=4,'dp_1'=4,'dp_2'=4,'dp_3'=2,'tensor'=2] {'dp_3'}, dimensions={0} | all-to-all | bytes 3670016 | tf_op jit(solution)/shard_map/all_to_all | solution.py:41
  410.4 1.5 copy.31
  411.9 9.3 %all-to-all-start.2 = ((f32[64,14,256]{2,1,0:T(8,128)}), f32[64,14,256]{2,1,0:T(8,128)S(1)}, u32[]{:S(2)}, u32[]{:S(2)}) async-start(f32[64,14,256]{2,1,0:T(8,128)} %copy.31), calls=%async_computation.2 | async-start | bytes 2097152 | tf_op jit(solution)/shard_map/all_to_all | solution.py:48
  423.1 26.9 %all-reduce.2 = (f32[]{:T(128)}, f32[]{:T(128)}) all-reduce(f32[]{:T(128)S(6)} %mul.184, f32[]{:T(128)S(6)} %mul.191), channel_id=1, replica_groups=mesh['dp_0'=4,'dp_1'=4,'dp_2'=4,'dp_3'=2,'tensor'=2] {'dp_0'}, use_global_device_ids=true, to_apply=%region_5.0 | all-reduce | flops 2 | bytes 16 | tf_op jit(solution)/shard_map/psum | solution.py:53
  450.1 8.9 %all-reduce.1 = (f32[]{:T(128)}, f32[]{:T(128)}) all-reduce(f32[]{:T(128)} %get-tuple-element.7, f32[]{:T(128)} %get-tuple-element.8), channel_id=1, replica_groups=mesh['dp_0'=4,'dp_1'=4,'dp_2'=4,'dp_3'=2,'tensor'=2] {'dp_1'}, use_global_device_ids=true, to_apply=%region_6.0 | all-reduce | flops 2 | bytes 16 | tf_op jit(solution)/shard_map/psum | solution.py:53
  459.0 8.8 %all-reduce = (f32[]{:T(128)}, f32[]{:T(128)}) all-reduce(f32[]{:T(128)} %get-tuple-element.5, f32[]{:T(128)} %get-tuple-element.6), channel_id=1, replica_groups=mesh['dp_0'=4,'dp_1'=4,'dp_2'=4,'dp_3'=2,'tensor'=2] {'dp_2'}, use_global_device_ids=true, to_apply=%region_7.0 | all-reduce | flops 2 | bytes 16 | tf_op jit(solution)/shard_map/psum | solution.py:53
  467.8 8.8 %all-reduce.4 = (f32[]{:T(128)}, f32[]{:T(128)}) all-reduce(f32[]{:T(128)} %get-tuple-element.3, f32[]{:T(128)} %get-tuple-element.4), channel_id=1, replica_groups=mesh['dp_0'=4,'dp_1'=4,'dp_2'=4,'dp_3'=2,'tensor'=2] {'dp_3'}, use_global_device_ids=true, to_apply=%region_8.0 | all-reduce | flops 2 | bytes 16 | tf_op jit(solution)/shard_map/psum | solution.py:53
  476.5 4.6 all-reduce.3
  482.7 1.3 fusion.39
  (28 shorter events, 4.7 us)
Async XLA Ops:
  7.2 152.6 %copy-start = (bf16[128,1792]{1,0:T(8,128)(2,1)S(1)}, bf16[128,1792]{1,0:T(8,128)(2,1)}, u32[]{:S(2)}) copy-start(bf16[128,1792]{1,0:T(8,128)(2,1)} %param.8) | copy-start | bytes 1376260
  7.2 117.9 %all-gather.5.cloned.1.call-start = ((), (), s32[]{:S(2)}) async-start(), calls=%async_computation.3 | async-start | bytes 14794752 | tf_op jit(solution)/shard_map/all_gather | solution.py:92
  7.9 227.9 %all-gather.7.cloned.1.call-start = ((), (), s32[]{:S(2)}) async-start(), calls=%async_computation.4 | async-start | bytes 14794752 | tf_op jit(solution)/shard_map/all_gather | solution.py:96
  263.3 5.7 %copy-start.5 = (s32[128]{0:T(128)S(1)}, s32[128]{0:T(128)}, u32[]{:S(2)}) copy-start(s32[128]{0:T(128)} %param.10) | copy-start | bytes 1540
  263.3 47.2 %all-to-all-start = ((f32[2,1,458752]{2,1,0:T(1,128)}), f32[2,1,458752]{2,1,0:T(1,128)}, u32[]{:S(2)}, u32[]{:S(2)}) async-start(f32[2,1,458752]{2,1,0:T(1,128)} %broadcast_in_dim.2), calls=%async_computation | async-start | bytes 7340032 | tf_op jit(solution)/shard_map/all_to_all | solution.py:17
  333.1 6.7 %copy-start.2 = (f32[128,7168]{1,0:T(8,128)S(1)}, f32[128,7168]{1,0:T(8,128)}, u32[]{:S(2)}) copy-start(f32[128,7168]{1,0:T(8,128)} %fusion.10) | copy-start | bytes 11010052
  333.1 6.7 %copy-start.3 = (s32[3584]{0:T(1024)S(1)}, s32[3584]{0:T(1024)}, u32[]{:S(2)}) copy-start(s32[3584]{0:T(1024)} %param.14) | copy-start | bytes 43012
  404.1 79.9 %copy-start.1 = (bf16[128,1792]{1,0:T(8,128)(2,1)S(1)}, bf16[128,1792]{1,0:T(8,128)(2,1)}, u32[]{:S(2)}) copy-start(bf16[128,1792]{1,0:T(8,128)(2,1)} %param.8) | copy-start | bytes 1376260
  410.2 72.5 %copy-start.4 = (f32[14,256]{1,0:T(8,128)S(1)}, f32[14,256]{1,0:T(8,128)}, u32[]{:S(2)}) copy-start(f32[14,256]{1,0:T(8,128)} %param.15) | copy-start | bytes 43012
  411.9 70.6 %all-to-all-start.2 = ((f32[64,14,256]{2,1,0:T(8,128)}), f32[64,14,256]{2,1,0:T(8,128)S(1)}, u32[]{:S(2)}, u32[]{:S(2)}) async-start(f32[64,14,256]{2,1,0:T(8,128)} %copy.31), calls=%async_computation.2 | async-start | bytes 2097152 | tf_op jit(solution)/shard_map/all_to_all | solution.py:48
Sparse Core Ops, SparseCore 0:
  11.4 113.6 all-gather.4
  128.5 107.3 all-gather.6
where the time goes:
time: 495 us; the launch traced here: 492 us
  waiting for transfers between devices  200 us (40%)
  local copies, waits for them, and re-layouts  90.2 us (18%)
  blocking collectives  64.2 us (13%)
  other arithmetic  57.6 us (12%)
  matrix products  46.8 us (9%)
  between operations  18 us (4%)
  starting transfers between devices  15.1 us (3%)
    all_gather x1, waiting for transfers between devices, body(): lax.all_gather(up_weight, DP, axis=0, tiled=True)  99.8 us
    psum x5, blocking collectives, one_axis_at_a_time(): shard = lax.psum(shard, axis)  58.1 us
    all_gather x1, waiting for transfers between devices, body(): full_down = lax.all_gather(down_weight, DP, axis=0, tiled=True)  57.5 us
    unnamed x15, local copies, waits for them, and re-layouts  51.6 us
    all_to_all x1, waiting for transfers between devices, sent_to_all(): return lax.all_to_all(copies, axis, split_axis=0, concat_axis=0, tiled=True)  41.4 us
    reshape x1, local copies, waits for them, and re-layouts, body(): hutch_terms.reshape(own_rows * lax.axis_size(DP), ff_local // BLOCK, BLOCK)  26.7 us
    reduce_sum x1, other arithmetic, over_copies(): return jnp.sum(everything, axis=0)  18.1 us
    dot_general x1, matrix products, body(): jnp.einsum('tr,tf->rf', columns, chain_grad, preferred_element_type=jnp.f...  17.9 us
  transfers between devices with their start and end apart: 4, of which 3 were waited for; matrix products, arithmetic and copies ran while one was open for 14% of the time, Pallas kernels for 0%

commit v1 on v0

--- a/solution.py
+++ b/solution.py
@@ -50,7 +50,7 @@
 
 def one_axis_at_a_time(shard, axes):
     for axis in axes:
-        shard = lax.psum(shard, axis)
+        shard = jnp.sum(lax.all_gather(shard, axis), axis=0)
     return shard
 
 

time: 495 us -> 511 us (1.032)
  local copies, waits for them, and re-layouts: 90.2 us -> 106 us
  other arithmetic: 57.6 us -> 63.7 us
  blocking collectives: 64.2 us -> 58.1 us
    psum x5 -> x0, blocking collectives: 58.1 us -> none  [one_axis_at_a_time(): shard = lax.psum(shard, axis)]
    unnamed x0 -> x5, blocking collectives: none -> 52 us
    unnamed x15 -> x50, local copies, waits for them, and re-layouts: 51.6 us -> 67.5 us
    reduce_sum x0 -> x10, other arithmetic: none -> 6.09 us  [one_axis_at_a_time(): shard = jnp.sum(lax.all_gather(shard, axis), axis=0)]
  transfers between devices with their start and end apart: 4 -> 4, of which waited for: 3 -> 3; matrix products, arithmetic and copies ran while one was open for 14% -> 18% of each run, Pallas kernels for 0% -> 0%
where the time goes in v1:
time: 511 us; the launch traced here: 508 us
  waiting for transfers between devices  200 us (39%)
  local copies, waits for them, and re-layouts  106 us (21%)
  other arithmetic  63.7 us (12%)
  blocking collectives  58.1 us (11%)
  matrix products  46.8 us (9%)
  between operations  18.1 us (4%)
  starting transfers between devices  15.1 us (3%)
    all_gather x1, waiting for transfers between devices, body(): lax.all_gather(up_weight, DP, axis=0, tiled=True)  99.8 us
    unnamed x50, local copies, waits for them, and re-layouts  67.5 us
    all_gather x1, waiting for transfers between devices, body(): full_down = lax.all_gather(down_weight, DP, axis=0, tiled=True)  57.5 us
    unnamed x5, blocking collectives  52 us
    all_to_all x1, waiting for transfers between devices, sent_to_all(): return lax.all_to_all(copies, axis, split_axis=0, concat_axis=0, tiled=True)  41.4 us
    reshape x1, local copies, waits for them, and re-layouts, body(): hutch_terms.reshape(own_rows * lax.axis_size(DP), ff_local // BLOCK, BLOCK)  26.7 us
    reduce_sum x1, other arithmetic, over_copies(): return jnp.sum(everything, axis=0)  18.1 us
    dot_general x1, matrix products, body(): jnp.einsum('tr,tf->rf', columns, chain_grad, preferred_element_type=jnp.f...  17.9 us
  transfers between devices with their start and end apart: 4, of which 3 were waited for; matrix products, arithmetic and copies ran while one was open for 18% of the time, Pallas kernels for 0%

profile of v1, /device:TPU:1, one launch (start us, length us, event | category | flops | bytes accessed | tf_op | source)
XLA Modules:
  0.0 507.9 jit_solution(455806636902004560)
XLA Ops:
  9.4 15.8 %add_convert_fusion = bf16[1792,3584]{0,1:T(8,128)(2,1)} fusion(s32[3584]{0:T(1024)} %param.14, s32[1792]{0:T(1024)S(1)} %broadcast_multiply_fusion.1), kind=kLoop, calls=%fused_computation.13 | loop fusion | flops 109182976 | bytes 12866560 | tf_op jit(solution)/shard_map/convert_element_type | solution.py:65
  25.2 99.8 %all-gather.5.cloned.1.call-done = bf16[128,14,3584]{2,1,0:T(8,128)(2,1)} async-done(((bf16[1,14,3584]{2,1,0:T(8,128)(2,1)}), bf16[128,14,3584]{2,1,0:T(8,128)(2,1)}) %all-gather.5.cloned.1.call-update) | async-done | bytes 12845072 | tf_op jit(solution)/shard_map/all_gather | solution.py:92
  125.0 16.8 %reshape.78 = bf16[1792,3584]{1,0:T(8,128)(2,1)} reshape(bf16[128,14,3584]{2,1,0:T(8,128)(2,1)} %all-gather.5.cloned.1.call-done) | data formatting | bytes 25690112
  141.9 17.9 %copy.27 = bf16[1792,3584]{0,1:T(8,128)(2,1)} copy(bf16[1792,3584]{1,0:T(8,128)(2,1)} %reshape.78) | data formatting | bytes 25690112
  159.8 15.2 %fusion.10 = f32[128,7168]{1,0:T(8,128)} fusion(bf16[128,1792]{1,0:T(8,128)(2,1)S(1)} %copy-done, bf16[1792,3584]{0,1:T(8,128)(2,1)} %add_convert_fusion, bf16[1792,3584]{0,1:T(8,128)(2,1)} %copy.27), kind=kOutput, calls=%fused_computation.14 | convolution fusion | flops 3339714560 | bytes 29818880 | tf_op jit(solution)/shard_map/dot_general | solution.py:93
  175.0 3.3 multiply_convert_fusion.1
  178.3 57.5 %all-gather.7.cloned.1.call-done = bf16[128,14,3584]{2,1,0:T(8,128)(2,1)} async-done(((bf16[1,14,3584]{2,1,0:T(8,128)(2,1)}), bf16[128,14,3584]{2,1,0:T(8,128)(2,1)}) %all-gather.7.cloned.1.call-update) | async-done | bytes 12845072 | tf_op jit(solution)/shard_map/all_gather | solution.py:96
  235.8 16.8 %reshape.80 = bf16[1792,3584]{1,0:T(8,128)(2,1)} reshape(bf16[128,14,3584]{2,1,0:T(8,128)(2,1)} %all-gather.7.cloned.1.call-done) | data formatting | bytes 25690112
  252.6 7.0 %fusion.23 = f32[256,1792]{1,0:T(8,128)S(1)} fusion(bf16[1792,3584]{1,0:T(8,128)(2,1)} %reshape.80, bf16[128,3584]{1,0:T(8,128)(2,1)S(1)} %get-tuple-element.16, bf16[128,3584]{1,0:T(8,128)(2,1)S(1)} %get-tuple-element.15), kind=kOutput, calls=%fused_computation.29 | convolution fusion | flops 3292004352 | bytes 16515072 | tf_op jit(solution)/shard_map/tf,df->td/dot_general | solution.py:101
  260.1 3.3 broadcast_in_dim.2
  263.3 5.7 %all-to-all-start = ((f32[2,1,458752]{2,1,0:T(1,128)}), f32[2,1,458752]{2,1,0:T(1,128)}, u32[]{:S(2)}, u32[]{:S(2)}) async-start(f32[2,1,458752]{2,1,0:T(1,128)} %broadcast_in_dim.2), calls=%async_computation | async-start | bytes 7340032 | tf_op jit(solution)/shard_map/all_to_all | solution.py:17
  269.1 41.4 %all-to-all-done = f32[2,1,458752]{2,1,0:T(1,128)} async-done(((f32[2,1,458752]{2,1,0:T(1,128)}), f32[2,1,458752]{2,1,0:T(1,128)}, u32[]{:S(2)}, u32[]{:S(2)}) %all-to-all-start) | async-done | bytes 3670048 | tf_op jit(solution)/shard_map/all_to_all | solution.py:17
  310.5 18.1 %reduce_sum.144 = f32[458752]{0:T(1024)S(1)} reduce(f32[2,1,458752]{2,1,0:T(1,128)} %all-to-all-done, f32[]{:T(128)} %constant.20.clone.1), dimensions={0,1}, to_apply=%region_0.0 | reduce | flops 458752 | bytes 5505028 | tf_op jit(solution)/shard_map/reduce_sum | solution.py:22
  331.2 2.0 fusion.27
  333.1 6.7 %fusion.29 = f32[256,3584]{1,0:T(8,128)S(1)} fusion(bf16[1792,3584]{1,0:T(8,128)(2,1)} %reshape.80, bf16[128,1792]{1,0:T(8,128)(2,1)S(1)} %get-tuple-element.23, bf16[128,1792]{1,0:T(8,128)(2,1)S(1)} %get-tuple-element.22), kind=kOutput, calls=%fused_computation.41 | convolution fusion | flops 3290169344 | bytes 17432576 | tf_op jit(solution)/shard_map/dot_general | solution.py:108
  339.8 17.9 %bitcast_multiply_fusion = f32[1792,3584]{0,1:T(8,128)} fusion(bf16[128,1792]{1,0:T(8,128)(2,1)S(1)} %copy-done, s32[3584]{0:T(1024)S(1)} %copy-done.3, s32[1792]{0:T(1024)S(1)} %broadcast_multiply_fusion.1, f32[256,3584]{1,0:T(8,128)S(1)} %fusion.29, f32[128,7168]{1,0:T(8,128)S(1)} %copy-done.2), kind=kOutput, calls=%fused_computation.12 | convolution fusion | flops 1779957760 | bytes 33510400 | tf_op jit(solution)/shard_map/tr,tf->rf/dot_general | solution.py:117
  357.7 26.7 %reshape.46 = f32[1792,256,14]{0,2,1:T(8,128)} reshape(f32[1792,3584]{0,1:T(8,128)} %bitcast_multiply_fusion) | data formatting | bytes 51380224 | tf_op jit(solution)/shard_map/reshape | solution.py:121
  384.4 13.6 %reduce_sum.145 = f32[1792,256]{0,1:T(8,128)} reduce(f32[1792,256,14]{0,2,1:T(8,128)} %reshape.46, f32[]{:T(128)} %constant.20.clone.1), dimensions={2}, to_apply=%region_1.0 | reduce | flops 5963776 | bytes 27525124 | tf_op jit(solution)/shard_map/reduce_sum | solution.py:121
  398.0 1.7 broadcast_multiply_fusion
  399.7 1.7 copy.29
  401.4 1.6 div.19
  404.1 6.1 %all_to_all.16 = f32[2,64,14,256]{3,1,2,0:T(8,128)S(1)} all-to-all(f32[2,64,14,256]{3,1,2,0:T(8,128)S(1)} %copy.30), channel_id=1, replica_groups=mesh['dp_0'=4,'dp_1'=4,'dp_2'=4,'dp_3'=2,'tensor'=2] {'dp_3'}, dimensions={0} | all-to-all | bytes 3670016 | tf_op jit(solution)/shard_map/all_to_all | solution.py:41
  410.4 1.5 copy.31
  412.0 9.3 %all-to-all-start.2 = ((f32[64,14,256]{2,1,0:T(8,128)}), f32[64,14,256]{2,1,0:T(8,128)S(1)}, u32[]{:S(2)}, u32[]{:S(2)}) async-start(f32[64,14,256]{2,1,0:T(8,128)} %copy.31), calls=%async_computation.2 | async-start | bytes 2097152 | tf_op jit(solution)/shard_map/all_to_all | solution.py:48
  426.1 23.5 %all-reduce.12 = (f32[4]{0:T(128)S(1)}, f32[4]{0:T(128)S(1)}) all-reduce(f32[4]{0:T(128)S(1)} %dynamic-update-slice, f32[4]{0:T(128)S(1)} %dynamic-update-slice.5), channel_id=1, replica_groups=mesh['dp_0'=4,'dp_1'=4,'dp_2'=4,'dp_3'=2,'tensor'=2] {'dp_0'}, use_global_device_ids=true, to_apply=%add | all-reduce | flops 8 | bytes 64
  452.2 1.4 dynamic-update-slice.6
  454.2 8.3 %all-reduce.11 = (f32[4]{0:T(128)S(1)}, f32[4]{0:T(128)S(1)}) all-reduce(f32[4]{0:T(128)S(1)} %dynamic-update-slice.1, f32[4]{0:T(128)S(1)} %dynamic-update-slice.6), channel_id=1, replica_groups=mesh['dp_0'=4,'dp_1'=4,'dp_2'=4,'dp_3'=2,'tensor'=2] {'dp_1'}, use_global_device_ids=true, to_apply=%add.1 | all-reduce | flops 8 | bytes 64
  467.1 8.1 %all-reduce.10 = (f32[4]{0:T(128)S(1)}, f32[4]{0:T(128)S(1)}) all-reduce(f32[4]{0:T(128)S(1)} %dynamic-update-slice.2, f32[4]{0:T(128)S(1)} %dynamic-update-slice.7), channel_id=1, replica_groups=mesh['dp_0'=4,'dp_1'=4,'dp_2'=4,'dp_3'=2,'tensor'=2] {'dp_2'}, use_global_device_ids=true, to_apply=%add.2 | all-reduce | flops 8 | bytes 64
  477.8 1.4 dynamic-update-slice.8
  479.8 8.1 %all-reduce.14 = (f32[2]{0:T(128)S(1)}, f32[2]{0:T(128)S(1)}) all-reduce(f32[2]{0:T(128)S(1)} %dynamic-update-slice.3, f32[2]{0:T(128)S(1)} %dynamic-update-slice.8), channel_id=1, replica_groups=mesh['dp_0'=4,'dp_1'=4,'dp_2'=4,'dp_3'=2,'tensor'=2] {'dp_3'}, use_global_device_ids=true, to_apply=%add.3 | all-reduce | flops 4 | bytes 32
  490.5 1.4 dynamic-update-slice.9
  491.9 3.9 all-reduce.13
  (73 shorter events, 26.2 us)
Async XLA Ops:
  7.2 152.6 %copy-start = (bf16[128,1792]{1,0:T(8,128)(2,1)S(1)}, bf16[128,1792]{1,0:T(8,128)(2,1)}, u32[]{:S(2)}) copy-start(bf16[128,1792]{1,0:T(8,128)(2,1)} %param.8) | copy-start | bytes 1376260
  7.2 117.9 %all-gather.5.cloned.1.call-start = ((), (), s32[]{:S(2)}) async-start(), calls=%async_computation.3 | async-start | bytes 14794752 | tf_op jit(solution)/shard_map/all_gather | solution.py:92
  7.9 227.9 %all-gather.7.cloned.1.call-start = ((), (), s32[]{:S(2)}) async-start(), calls=%async_computation.4 | async-start | bytes 14794752 | tf_op jit(solution)/shard_map/all_gather | solution.py:96
  263.3 5.7 %copy-start.5 = (s32[128]{0:T(128)S(1)}, s32[128]{0:T(128)}, u32[]{:S(2)}) copy-start(s32[128]{0:T(128)} %param.10) | copy-start | bytes 1540
  263.3 47.2 %all-to-all-start = ((f32[2,1,458752]{2,1,0:T(1,128)}), f32[2,1,458752]{2,1,0:T(1,128)}, u32[]{:S(2)}, u32[]{:S(2)}) async-start(f32[2,1,458752]{2,1,0:T(1,128)} %broadcast_in_dim.2), calls=%async_computation | async-start | bytes 7340032 | tf_op jit(solution)/shard_map/all_to_all | solution.py:17
  333.1 6.7 %copy-start.2 = (f32[128,7168]{1,0:T(8,128)S(1)}, f32[128,7168]{1,0:T(8,128)}, u32[]{:S(2)}) copy-start(f32[128,7168]{1,0:T(8,128)} %fusion.10) | copy-start | bytes 11010052
  333.1 6.7 %copy-start.3 = (s32[3584]{0:T(1024)S(1)}, s32[3584]{0:T(1024)}, u32[]{:S(2)}) copy-start(s32[3584]{0:T(1024)} %param.14) | copy-start | bytes 43012
  404.1 95.9 %copy-start.1 = (bf16[128,1792]{1,0:T(8,128)(2,1)S(1)}, bf16[128,1792]{1,0:T(8,128)(2,1)}, u32[]{:S(2)}) copy-start(bf16[128,1792]{1,0:T(8,128)(2,1)} %param.8) | copy-start | bytes 1376260
  410.2 12.3 %copy-start.10 = (u32[256]{0:T(256)S(1)}, u32[256]{0:T(256)}, u32[]{:S(2)}) copy-start(u32[256]{0:T(256)} %constant.55) | copy-start | bytes 3076
  410.2 15.3 %copy-start.9 = (u32[256]{0:T(256)S(1)}, u32[256]{0:T(256)}, u32[]{:S(2)}) copy-start(u32[256]{0:T(256)} %constant.60) | copy-start | bytes 3076
  410.2 43.4 %copy-start.8 = (u32[256]{0:T(256)S(1)}, u32[256]{0:T(256)}, u32[]{:S(2)}) copy-start(u32[256]{0:T(256)} %constant.65) | copy-start | bytes 3076
  410.2 56.3 %copy-start.7 = (u32[256]{0:T(256)S(1)}, u32[256]{0:T(256)}, u32[]{:S(2)}) copy-start(u32[256]{0:T(256)} %constant.70) | copy-start | bytes 3076
  410.2 69.0 %copy-start.6 = (u32[256]{0:T(256)S(1)}, u32[256]{0:T(256)}, u32[]{:S(2)}) copy-start(u32[256]{0:T(256)} %constant.75) | copy-start | bytes 3076
  410.2 88.4 %copy-start.4 = (f32[14,256]{1,0:T(8,128)S(1)}, f32[14,256]{1,0:T(8,128)}, u32[]{:S(2)}) copy-start(f32[14,256]{1,0:T(8,128)} %param.15) | copy-start | bytes 43012
  412.0 86.6 %all-to-all-start.2 = ((f32[64,14,256]{2,1,0:T(8,128)}), f32[64,14,256]{2,1,0:T(8,128)S(1)}, u32[]{:S(2)}, u32[]{:S(2)}) async-start(f32[64,14,256]{2,1,0:T(8,128)} %copy.31), calls=%async_computation.2 | async-start | bytes 2097152 | tf_op jit(solution)/shard_map/all_to_all | solution.py:48
Sparse Core Ops, SparseCore 0:
  11.4 113.6 all-gather.4
  128.5 107.3 all-gather.6
